TPU v7x, 256 devices: a whole 4x4x8 slice. The times are simulated.
256 devices in a mesh: seq: 64 (over x, z, core), grp: 4 (over y).
Axes of the slice: x: 4, y: 4, z: 8, core: 2. Of those that a mesh axis runs over, the one named last changes fastest.
Arguments:
- delta_codes: int32 [16, 16, 16384, 128], P('grp', None, 'seq'), may hold values from -63 to 63, as said below
- scale_index: int32 [16, 16, 1024], P('grp', None, 'seq'), may hold values from 0 to 15
- anchor_codes: int32 [16, 16, 128], P('grp'), may hold values from -8 to 7
- scale_table: float32 [16, 128], replicated, may hold values from 5e-05 to 0.0005
- anchor_scale: float32 [128], replicated, may hold values from 0.0001 to 0.001
Outputs:
- decode_cache: bfloat16 [4, 64, 16384, 128], P('grp', 'seq')
Inputs may be any that keep to these rules, and one draw needn't show every extreme that they name: `delta_codes`: for every sequence, head and channel, the running sum of the codes from the sequence's first token lies in -32 .. 31 after every token, and in -2 .. 1 after the last token of each group of 16 tokens.
All inputs are finite; a program needn't handle non-finite values.
Results may differ from a plain program's by a relative error of at most 0.001.
Values may be sent and summed in bfloat16 or wider, within the bound.
A program may use at most 128 MiB of HBM per device.

v0:
```python
import jax
import jax.numpy as jnp
from jax import lax
from jax.sharding import PartitionSpec as P


def lookup_scales(scale_ids, scale_table):
    levels = scale_table.shape[0]
    onehot = (scale_ids[..., None] == jnp.arange(levels, dtype=jnp.int32)).astype(jnp.float32)
    flat = jnp.dot(
        onehot.reshape(-1, levels),
        scale_table,
        precision=lax.Precision.HIGHEST,
        preferred_element_type=jnp.float32,
    )
    return flat.reshape(scale_ids.shape + (scale_table.shape[1],))


def dequantize(code_vals, scale_ids, scale_table):
    head_dim = code_vals.shape[-1]
    steps_len = code_vals.shape[-2]
    groups = scale_ids.shape[-1]
    scales = lookup_scales(scale_ids, scale_table)
    lead_dims = code_vals.shape[:-2]
    shaped = code_vals.astype(jnp.float32).reshape(
        lead_dims + (groups, steps_len // groups, head_dim)
    )
    return (shaped * scales[..., :, None, :]).reshape(code_vals.shape)


def block_prefix(deltas):
    tok_len = deltas.shape[1]
    lower_ones = (jnp.arange(tok_len)[:, None] >= jnp.arange(tok_len)[None, :]).astype(jnp.float32)
    return jnp.einsum("tu,ruc->rtc", lower_ones, deltas, precision=lax.Precision.HIGHEST)


def finish_rows(prefix_rows, totals, seq_count):
    strict = (jnp.arange(seq_count)[:, None] > jnp.arange(seq_count)[None, :]).astype(jnp.float32)
    carried = jnp.einsum("ij,rjc->ric", strict, totals, precision=lax.Precision.HIGHEST)
    row_count, length, head_dim = prefix_rows.shape
    shaped = (
        prefix_rows.reshape(row_count, seq_count, length // seq_count, head_dim)
        + carried[:, :, None, :]
    )
    return shaped.astype(jnp.bfloat16).reshape(row_count, length, head_dim)


def on_device(delta_codes, scale_index, anchor_codes, scale_table, anchor_scale):
    seq_count = lax.axis_size("seq")
    seq_local, kv_heads, tok_dev, head_dim = delta_codes.shape
    packed = (
        delta_codes.astype(jnp.bfloat16),
        scale_index.astype(jnp.bfloat16),
        anchor_codes.astype(jnp.bfloat16),
    )
    sectioned = (
        lax.all_to_all(packed[0], "grp", split_axis=1, concat_axis=0, tiled=True),
        lax.all_to_all(packed[1], "grp", split_axis=1, concat_axis=0, tiled=True),
        lax.all_to_all(packed[2], "grp", split_axis=1, concat_axis=0, tiled=True),
    )
    code_rows = sectioned[0].reshape(-1, tok_dev, head_dim)
    id_rows = sectioned[1].reshape(code_rows.shape[0], -1)
    anchor_rows = sectioned[2].reshape(code_rows.shape[0], head_dim)
    moved = (
        lax.all_to_all(code_rows, "seq", split_axis=0, concat_axis=1, tiled=True),
        lax.all_to_all(id_rows, "seq", split_axis=0, concat_axis=1, tiled=True),
    )
    row_count = moved[0].shape[0]
    start = lax.axis_index("seq") * row_count
    my_anchor = lax.dynamic_slice_in_dim(anchor_rows, start, row_count, 0)
    anchor_vals = my_anchor.astype(jnp.float32) * anchor_scale
    deltas = dequantize(moved[0], moved[1].astype(jnp.int32), scale_table)
    prefix = block_prefix(deltas.reshape(-1, tok_dev, head_dim)).reshape(
        row_count, seq_count, tok_dev, head_dim
    )
    totals = prefix[:, :, -1, :]
    prefix_rows = (prefix + anchor_vals[:, None, None, :]).reshape(row_count, -1, head_dim)
    result = finish_rows(prefix_rows, totals, seq_count)
    return result[None]


def solution(mesh):
    placed = (P("grp", None, "seq", None), P("grp", None, "seq"), P("grp", None, None), P(), P())
    return jax.shard_map(
        on_device,
        mesh=mesh,
        in_specs=placed,
        out_specs=P("grp", "seq", None, None),
        check_vma=False,
    )
```

profile of v0, /device:TPU:1, one launch (start us, length us, event | category | flops | bytes accessed | tf_op | source)
XLA Modules:
  0.0 227.8 jit_solution(3346207164019680870)
XLA Ops:
  0.0 0.0 copy-start
  0.0 0.8 fusion.8
  0.8 0.1 reshape.92
  0.9 8.9 %all_to_all.67 = bf16[4,2,128]{2,1,0:T(2,128)(2,1)S(1)} all-to-all(bf16[4,2,128]{2,1,0:T(2,128)(2,1)S(1)} %reshape.92), channel_id=1, replica_groups=mesh['seq'=64,'grp'=4] {'grp'}, dimensions={0} | all-to-all | bytes 4096 | tf_op jit(solution)/shard_map/all_to_all | solution.py:58
  9.8 0.1 reshape.93
  9.9 0.6 copy.17
  10.5 13.6 %all-to-all-start.3 = ((bf16[64,1,16]{2,1,0:T(2,128)(2,1)}), bf16[64,1,16]{2,1,0:T(2,128)(2,1)S(1)}, u32[]{:S(2)}, u32[]{:S(2)}) async-start(bf16[64,1,16]{2,1,0:T(2,128)(2,1)} %copy.17), calls=%async_computation.3 | async-start | bytes 65536 | tf_op jit(solution)/shard_map/all_to_all | solution.py:66
  24.1 0.0 copy-start.1
  24.1 6.4 %copy_convert_fusion = bf16[4,16,256,128]{3,2,0,1:T(8,128)(2,1)} fusion(s32[4,16,256,128]{3,2,1,0:T(8,128)} %param.5), kind=kLoop, calls=%fused_computation.4 | loop fusion | flops 2097152 | bytes 12582912 | tf_op jit(solution)/shard_map/convert_element_type | solution.py:52
  30.5 2.9 %all-to-all-done.3 = bf16[64,1,16]{2,1,0:T(2,128)(2,1)S(1)} async-done(((bf16[64,1,16]{2,1,0:T(2,128)(2,1)}), bf16[64,1,16]{2,1,0:T(2,128)(2,1)S(1)}, u32[]{:S(2)}, u32[]{:S(2)}) %all-to-all-start.3) | async-done | bytes 2080 | tf_op jit(solution)/shard_map/all_to_all | solution.py:66
  33.4 4.8 %all-to-all-start = ((bf16[4,16,256,128]{3,2,0,1:T(8,128)(2,1)}), bf16[4,16,256,128]{3,2,0,1:T(8,128)(2,1)}, u32[]{:S(2)}, u32[]{:S(2)}) async-start(bf16[4,16,256,128]{3,2,0,1:T(8,128)(2,1)} %copy_convert_fusion), calls=%async_computation | async-start | bytes 8388608 | tf_op jit(solution)/shard_map/all_to_all | solution.py:57
  38.3 0.0 copy-done.1
  38.3 0.6 copy_convert_fusion.1
  38.9 47.7 %all-to-all-done = bf16[4,16,256,128]{3,2,0,1:T(8,128)(2,1)} async-done(((bf16[4,16,256,128]{3,2,0,1:T(8,128)(2,1)}), bf16[4,16,256,128]{3,2,0,1:T(8,128)(2,1)}, u32[]{:S(2)}, u32[]{:S(2)}) %all-to-all-start) | async-done | bytes 4194336 | tf_op jit(solution)/shard_map/all_to_all | solution.py:57
  86.6 3.2 %all-to-all-start.4 = ((bf16[4,16,128]{2,0,1:T(4,128)(2,1)}), bf16[4,16,128]{2,0,1:T(4,128)(2,1)S(1)}, u32[]{:S(2)}, u32[]{:S(2)}) async-start(bf16[4,16,128]{2,0,1:T(4,128)(2,1)} %copy_convert_fusion.1), calls=%async_computation.4 | async-start | bytes 32768 | tf_op jit(solution)/shard_map/all_to_all | solution.py:59
  89.8 0.0 copy-start.2
  89.8 4.7 %copy.14 = bf16[4,4,4,256,128]{4,3,2,0,1:T(8,128)(2,1)} copy(bf16[4,4,4,256,128]{4,3,0,2,1:T(8,128)(2,1)} %bitcast) | data formatting | bytes 8388608 | tf_op jit(solution)/shard_map/all_to_all | solution.py:57
  94.6 0.0 all-to-all-done.4
  94.6 9.3 %all-to-all-start.1 = ((bf16[64,256,128]{2,1,0:T(8,128)(2,1)}), bf16[64,256,128]{2,1,0:T(8,128)(2,1)}, u32[]{:S(2)}, u32[]{:S(2)}) async-start(bf16[64,256,128]{2,1,0:T(8,128)(2,1)} %bitcast.47), calls=%async_computation.1 | async-start | bytes 8388608 | tf_op jit(solution)/shard_map/all_to_all | solution.py:65
  103.9 0.1 convert_reduce_fusion
  104.0 0.1 reshape.82
  104.1 0.0 copy-done
  104.1 0.5 fusion.2
  104.6 0.0 copy-done.2
  104.6 95.1 %all-to-all-done.1 = bf16[64,256,128]{2,1,0:T(8,128)(2,1)} async-done(((bf16[64,256,128]{2,1,0:T(8,128)(2,1)}), bf16[64,256,128]{2,1,0:T(8,128)(2,1)}, u32[]{:S(2)}, u32[]{:S(2)}) %all-to-all-start.1) | async-done | bytes 4194336 | tf_op jit(solution)/shard_map/all_to_all | solution.py:65
  199.8 0.5 mul.16
  200.3 6.7 %bitcast_multiply_fusion = f32[64,256,128]{2,1,0:T(8,128)} fusion(bf16[64,256,128]{2,1,0:T(8,128)(2,1)} %all-to-all-done.1, f32[64,256,128]{2,1,0:T(8,128)S(1)} %bitcast.46), kind=kLoop, calls=%fused_computation.3 | loop fusion | flops 4194304 | bytes 20971520 | tf_op jit(solution)/shard_map/mul | solution.py:28
  207.0 9.4 %fusion.5 = f32[64,128,256]{2,1,0:T(8,128)S(1)} fusion(f32[64,256,128]{2,1,0:T(8,128)} %bitcast_multiply_fusion), kind=kOutput, calls=%fused_computation.12 | convolution fusion | flops 6442516480 | bytes 16777216 | tf_op jit(solution)/shard_map/tu,ruc->rtc/dot_general | solution.py:34
  216.4 2.2 slice_reduce_fusion
  218.7 0.1 convolution_bitcast_fusion
  218.8 2.6 %fusion.1 = bf16[64,256,128]{1,2,0:T(8,128)(2,1)} fusion(f32[64,128,256]{2,1,0:T(8,128)S(1)} %fusion.5, f32[64,128]{1,0:T(8,128)S(1)} %convolution_bitcast_fusion, f32[128]{0:T(128)S(1)} %fusion.7), kind=kLoop, calls=%fused_computation.2 | loop fusion | flops 6291456 | bytes 12616192 | tf_op jit(solution)/shard_map/convert_element_type | solution.py:45
  221.5 6.4 %copy.21 = bf16[64,256,128]{2,1,0:T(8,128)(2,1)} copy(bf16[64,256,128]{1,2,0:T(8,128)(2,1)} %fusion.1) | data formatting | bytes 8388608 | tf_op jit(solution)/shard_map/convert_element_type | solution.py:45
  (3 shorter events, 0.0 us)
Async XLA Ops:
  0.0 104.1 %copy-start = (f32[16,128]{1,0:T(8,128)S(1)}, f32[16,128]{1,0:T(8,128)}, u32[]{:S(2)}) copy-start(f32[16,128]{1,0:T(8,128)} %param.8) | copy-start | bytes 24580
  10.5 22.9 %all-to-all-start.3 = ((bf16[64,1,16]{2,1,0:T(2,128)(2,1)}), bf16[64,1,16]{2,1,0:T(2,128)(2,1)S(1)}, u32[]{:S(2)}, u32[]{:S(2)}) async-start(bf16[64,1,16]{2,1,0:T(2,128)(2,1)} %copy.17), calls=%async_computation.3 | async-start | bytes 65536 | tf_op jit(solution)/shard_map/all_to_all | solution.py:66
  24.1 14.2 %copy-start.1 = (s32[4,16,128]{2,1,0:T(8,128)S(1)}, s32[4,16,128]{2,1,0:T(8,128)}, u32[]{:S(2)}) copy-start(s32[4,16,128]{2,1,0:T(8,128)} %param.7) | copy-start | bytes 98308
  33.4 53.1 %all-to-all-start = ((bf16[4,16,256,128]{3,2,0,1:T(8,128)(2,1)}), bf16[4,16,256,128]{3,2,0,1:T(8,128)(2,1)}, u32[]{:S(2)}, u32[]{:S(2)}) async-start(bf16[4,16,256,128]{3,2,0,1:T(8,128)(2,1)} %copy_convert_fusion), calls=%async_computation | async-start | bytes 8388608 | tf_op jit(solution)/shard_map/all_to_all | solution.py:57
  86.6 8.0 %all-to-all-start.4 = ((bf16[4,16,128]{2,0,1:T(4,128)(2,1)}), bf16[4,16,128]{2,0,1:T(4,128)(2,1)S(1)}, u32[]{:S(2)}, u32[]{:S(2)}) async-start(bf16[4,16,128]{2,0,1:T(4,128)(2,1)} %copy_convert_fusion.1), calls=%async_computation.4 | async-start | bytes 32768 | tf_op jit(solution)/shard_map/all_to_all | solution.py:59
  89.8 14.8 %copy-start.2 = (f32[128]{0:T(128)S(1)}, f32[128]{0:T(128)}, u32[]{:S(2)}) copy-start(f32[128]{0:T(128)} %param.9) | copy-start | bytes 1540
  94.6 105.2 %all-to-all-start.1 = ((bf16[64,256,128]{2,1,0:T(8,128)(2,1)}), bf16[64,256,128]{2,1,0:T(8,128)(2,1)}, u32[]{:S(2)}, u32[]{:S(2)}) async-start(bf16[64,256,128]{2,1,0:T(8,128)(2,1)} %bitcast.47), calls=%async_computation.1 | async-start | bytes 8388608 | tf_op jit(solution)/shard_map/all_to_all | solution.py:65
where the time goes:
time: 228 us
  waiting for transfers between devices  146 us (64%)
  starting transfers between devices  31 us (14%)
  other arithmetic  17.3 us (8%)
  local copies, waits for them, and re-layouts  14.8 us (6%)
  matrix products  9.98 us (4%)
  blocking collectives  8.93 us (4%)
    all_to_all x1, waiting for transfers between devices, on_device(): lax.all_to_all(code_rows, 'seq', split_axis=0, concat_axis=1, tiled=True)  95.1 us
    all_to_all x1, waiting for transfers between devices, on_device(): lax.all_to_all(packed[0], 'grp', split_axis=1, concat_axis=0, tiled=True)  47.7 us
    all_to_all x1, starting transfers between devices, on_device(): lax.all_to_all(id_rows, 'seq', split_axis=0, concat_axis=1, tiled=True)  13.6 us
    dot_general x1, matrix products, block_prefix(): jnp.einsum('tu,ruc->rtc', lower_ones, deltas, precision=lax.Precision.HIG...  9.38 us
    all_to_all x1, starting transfers between devices, on_device(): lax.all_to_all(code_rows, 'seq', split_axis=0, concat_axis=1, tiled=True)  9.35 us
    all_to_all x1, blocking collectives, on_device(): lax.all_to_all(packed[1], 'grp', split_axis=1, concat_axis=0, tiled=True)  8.93 us
    mul x1, other arithmetic, dequantize(): return (shaped * scales[..., :, None, :]).reshape(code_vals.shape)  6.73 us
    convert_element_type x1, other arithmetic, on_device(): delta_codes.astype(jnp.bfloat16)  6.38 us
  transfers between devices with their start and end apart: 4, of which 3 were waited for; matrix products, arithmetic and copies ran while one was open for 5% of the time, Pallas kernels for 0%

commit v1 on v0

--- a/solution.py
+++ b/solution.py
@@ -46,6 +46,15 @@
 
 
 def on_device(delta_codes, scale_index, anchor_codes, scale_table, anchor_scale):
+
+    def trace_modes_for(values, axis_no, out_dim):
+        mat_out = lax.axis_size("seq")
+        out_arr = jnp.split(values, mat_out, axis=axis_no)
+        everything = jnp.stack(out_arr, axis=0)
+        ready = lax.all_to_all(everything, "seq", 0, 0)
+        high = jnp.concatenate(ready, axis=out_dim)
+        return high
+
     seq_count = lax.axis_size("seq")
     seq_local, kv_heads, tok_dev, head_dim = delta_codes.shape
     packed = (
@@ -62,7 +71,7 @@
     id_rows = sectioned[1].reshape(code_rows.shape[0], -1)
     anchor_rows = sectioned[2].reshape(code_rows.shape[0], head_dim)
     moved = (
-        lax.all_to_all(code_rows, "seq", split_axis=0, concat_axis=1, tiled=True),
+        trace_modes_for(code_rows, 0, 1),
         lax.all_to_all(id_rows, "seq", split_axis=0, concat_axis=1, tiled=True),
     )
     row_count = moved[0].shape[0]

time: 228 us -> 259 us (1.14)
  local copies, waits for them, and re-layouts: 14.8 us -> 55 us
  blocking collectives: 8.93 us -> 0 us
  starting transfers between devices: 31 us -> 38.6 us
  other arithmetic: 17.3 us -> 10.6 us
    unnamed x8 -> x73, local copies, waits for them, and re-layouts: 0.19 us -> 41.2 us
    all_to_all x1 -> x0, blocking collectives: 8.93 us -> none  [on_device(): lax.all_to_all(packed[1], 'grp', split_axis=1, concat_axis=0, tiled=True)]
    all_to_all x1 -> x2, starting transfers between devices: 9.35 us -> 16.7 us  [the longest x1 11.7 us: trace_modes_for(): ready = lax.all_to_all(everything, 'seq', 0, 0)]
    mul x1 -> x0, other arithmetic: 6.73 us -> none  [dequantize(): return (shaped * scales[..., :, None, :]).reshape(code_vals.shape)]
    all_to_all x1, waiting for transfers between devices: 2.92 us -> 0.01 us  [on_device(): lax.all_to_all(id_rows, 'seq', split_axis=0, concat_axis=1, tiled=True)]
    all_to_all x1, waiting for transfers between devices: 0.01 us -> 2.7 us  [on_device(): lax.all_to_all(packed[2], 'grp', split_axis=1, concat_axis=0, tiled=True)]
    all_to_all x1 -> x2, waiting for transfers between devices: 95.1 us -> 95.1 us  [the longest x1 95.1 us: trace_modes_for(): ready = lax.all_to_all(everything, 'seq', 0, 0)]
  transfers between devices with their start and end apart: 4 -> 5, of which waited for: 3 -> 3; matrix products, arithmetic and copies ran while one was open for 5% -> 20% of each run, Pallas kernels for 0% -> 0%
where the time goes in v1:
time: 259 us
  waiting for transfers between devices  144 us (56%)
  local copies, waits for them, and re-layouts  55 us (21%)
  starting transfers between devices  38.6 us (15%)
  other arithmetic  10.6 us (4%)
  matrix products  10.1 us (4%)
    all_to_all x1, waiting for transfers between devices, trace_modes_for(): ready = lax.all_to_all(everything, 'seq', 0, 0)  95.1 us
    all_to_all x1, waiting for transfers between devices, on_device(): lax.all_to_all(packed[0], 'grp', split_axis=1, concat_axis=0, tiled=True)  46.2 us
    unnamed x73, local copies, waits for them, and re-layouts  41.2 us
    all_to_all x1, starting transfers between devices, on_device(): lax.all_to_all(id_rows, 'seq', split_axis=0, concat_axis=1, tiled=True)  13.8 us
    all_to_all x1, starting transfers between devices, trace_modes_for(): ready = lax.all_to_all(everything, 'seq', 0, 0)  11.7 us
    dot_general x1, matrix products, block_prefix(): jnp.einsum('tu,ruc->rtc', lower_ones, deltas, precision=lax.Precision.HIG...  9.5 us
    convert_element_type x1, other arithmetic, on_device(): delta_codes.astype(jnp.bfloat16)  6.37 us
    convert_element_type x1, local copies, waits for them, and re-layouts, finish_rows(): return shaped.astype(jnp.bfloat16).reshape(row_count, length, head_dim)  6.35 us
  transfers between devices with their start and end apart: 5, of which 3 were waited for; matrix products, arithmetic and copies ran while one was open for 20% of the time, Pallas kernels for 0%

profile of v1, /device:TPU:1, one launch (start us, length us, event | category | flops | bytes accessed | tf_op | source)
XLA Modules:
  0.0 258.6 jit_solution(14411382428957409668)
XLA Ops:
  0.0 0.8 fusion.9
  0.8 0.7 reshape.93
  1.5 5.0 %all-to-all-start.2 = ((bf16[4,2,128]{2,1,0:T(2,128)(2,1)}), bf16[4,2,128]{2,1,0:T(2,128)(2,1)S(1)}, u32[]{:S(2)}, u32[]{:S(2)}) async-start(bf16[4,2,128]{2,1,0:T(2,128)(2,1)} %reshape.93), calls=%async_computation.2 | async-start | bytes 4096 | tf_op jit(solution)/shard_map/all_to_all | solution.py:67
  6.5 6.4 %copy_convert_fusion = bf16[4,16,256,128]{3,2,0,1:T(8,128)(2,1)} fusion(s32[4,16,256,128]{3,2,1,0:T(8,128)} %param.5), kind=kLoop, calls=%fused_computation.5 | loop fusion | flops 2097152 | bytes 12582912 | tf_op jit(solution)/shard_map/convert_element_type | solution.py:61
  12.9 5.0 %all-to-all-start = ((bf16[4,16,256,128]{3,2,0,1:T(8,128)(2,1)}), bf16[4,16,256,128]{3,2,0,1:T(8,128)(2,1)}, u32[]{:S(2)}, u32[]{:S(2)}) async-start(bf16[4,16,256,128]{3,2,0,1:T(8,128)(2,1)} %copy_convert_fusion), calls=%async_computation | async-start | bytes 8388608 | tf_op jit(solution)/shard_map/all_to_all | solution.py:66
  18.6 0.6 copy.144
  19.2 46.2 %all-to-all-done = bf16[4,16,256,128]{3,2,0,1:T(8,128)(2,1)} async-done(((bf16[4,16,256,128]{3,2,0,1:T(8,128)(2,1)}), bf16[4,16,256,128]{3,2,0,1:T(8,128)(2,1)}, u32[]{:S(2)}, u32[]{:S(2)}) %all-to-all-start) | async-done | bytes 4194336 | tf_op jit(solution)/shard_map/all_to_all | solution.py:66
  65.4 13.8 %all-to-all-start.3 = ((bf16[64,1,16]{2,1,0:T(2,128)(2,1)}), bf16[64,1,16]{2,1,0:T(2,128)(2,1)S(1)}, u32[]{:S(2)}, u32[]{:S(2)}) async-start(bf16[64,1,16]{2,1,0:T(2,128)(2,1)} %copy.144), calls=%async_computation.3 | async-start | bytes 65536 | tf_op jit(solution)/shard_map/all_to_all | solution.py:75
  79.2 2.5 copy.140
  81.6 0.7 constant_dynamic-update-slice_fusion.63
  82.3 1.1 constant_dynamic-update-slice_fusion.62
  83.4 0.6 constant_dynamic-update-slice_fusion.61
  84.1 0.6 constant_dynamic-update-slice_fusion.60
  84.7 0.6 constant_dynamic-update-slice_fusion.59
  85.3 0.6 constant_dynamic-update-slice_fusion.58
  86.0 0.6 constant_dynamic-update-slice_fusion.57
  86.6 0.6 constant_dynamic-update-slice_fusion.56
  87.2 0.6 constant_dynamic-update-slice_fusion.55
  87.9 0.6 constant_dynamic-update-slice_fusion.54
  88.5 0.6 constant_dynamic-update-slice_fusion.53
  89.1 0.6 constant_dynamic-update-slice_fusion.52
  89.8 0.6 constant_dynamic-update-slice_fusion.51
  90.4 0.6 constant_dynamic-update-slice_fusion.50
  91.0 0.6 constant_dynamic-update-slice_fusion.49
  91.7 0.6 constant_dynamic-update-slice_fusion.48
  92.3 0.6 constant_dynamic-update-slice_fusion.47
  92.9 0.6 constant_dynamic-update-slice_fusion.46
  93.6 0.6 constant_dynamic-update-slice_fusion.45
  94.2 0.6 constant_dynamic-update-slice_fusion.44
  96.1 0.6 constant_dynamic-update-slice_fusion.41
  97.4 0.6 constant_dynamic-update-slice_fusion.39
  98.7 0.6 constant_dynamic-update-slice_fusion.37
  99.9 0.6 constant_dynamic-update-slice_fusion.35
  108.2 0.6 constant_dynamic-update-slice_fusion.22
  109.4 0.6 constant_dynamic-update-slice_fusion.20
  110.7 0.6 constant_dynamic-update-slice_fusion.18
  112.0 0.6 constant_dynamic-update-slice_fusion.16
  120.2 0.6 constant_dynamic-update-slice_fusion.3
  121.5 0.6 constant_dynamic-update-slice_fusion.1
  122.1 3.2 %all-to-all-start.4 = ((bf16[4,16,128]{2,0,1:T(4,128)(2,1)}), bf16[4,16,128]{2,0,1:T(4,128)(2,1)S(1)}, u32[]{:S(2)}, u32[]{:S(2)}) async-start(bf16[4,16,128]{2,0,1:T(4,128)(2,1)} %copy_convert_fusion.1), calls=%async_computation.4 | async-start | bytes 32768 | tf_op jit(solution)/shard_map/all_to_all | solution.py:68
  125.4 1.5 constant_dynamic-update-slice_fusion
  126.9 2.7 %all-to-all-done.4 = bf16[4,16,128]{2,0,1:T(4,128)(2,1)S(1)} async-done(((bf16[4,16,128]{2,0,1:T(4,128)(2,1)}), bf16[4,16,128]{2,0,1:T(4,128)(2,1)S(1)}, u32[]{:S(2)}, u32[]{:S(2)}) %all-to-all-start.4) | async-done | bytes 16416 | tf_op jit(solution)/shard_map/all_to_all | solution.py:68
  129.6 11.7 %all-to-all-start.1 = ((bf16[64,1,256,128]{3,2,1,0:T(8,128)(2,1)}), bf16[64,1,256,128]{3,2,1,0:T(8,128)(2,1)}, u32[]{:S(2)}, u32[]{:S(2)}) async-start(bf16[64,1,256,128]{3,2,1,0:T(8,128)(2,1)} %constant_dynamic-update-slice_fusion), calls=%async_computation.1 | async-start | bytes 8388608 | tf_op jit(solution)/shard_map/all_to_all | solution.py:54
  142.0 95.1 %all-to-all-done.1 = bf16[64,1,256,128]{3,2,1,0:T(8,128)(2,1)} async-done(((bf16[64,1,256,128]{3,2,1,0:T(8,128)(2,1)}), bf16[64,1,256,128]{3,2,1,0:T(8,128)(2,1)}, u32[]{:S(2)}, u32[]{:S(2)}) %all-to-all-start.1) | async-done | bytes 4194336 | tf_op jit(solution)/shard_map/all_to_all | solution.py:54
  237.6 9.5 %fusion = f32[64,128,256]{2,1,0:T(8,128)S(1)} fusion(f32[64,256,128]{2,1,0:T(8,128)S(1)} %bitcast.307, bf16[64,1,256,128]{3,2,1,0:T(8,128)(2,1)} %all-to-all-done.1), kind=kOutput, calls=%fused_computation.1 | convolution fusion | flops 6446710784 | bytes 20971520 | tf_op jit(solution)/shard_map/tu,ruc->rtc/dot_general | solution.py:34
  247.1 2.2 slice_reduce_fusion
  249.5 2.7 %fusion.2 = bf16[64,256,128]{1,2,0:T(8,128)(2,1)} fusion(f32[64,128,256]{2,1,0:T(8,128)S(1)} %fusion, f32[64,128]{1,0:T(8,128)S(1)} %convolution_bitcast_fusion, f32[128]{0:T(128)S(1)} %fusion.8), kind=kLoop, calls=%fused_computation.4 | loop fusion | flops 6291456 | bytes 12616192 | tf_op jit(solution)/shard_map/convert_element_type | solution.py:45
  252.2 6.4 %copy.148 = bf16[64,256,128]{2,1,0:T(8,128)(2,1)} copy(bf16[64,256,128]{1,2,0:T(8,128)(2,1)} %fusion.2) | data formatting | bytes 8388608 | tf_op jit(solution)/shard_map/convert_element_type | solution.py:45
  (53 shorter events, 23.0 us)
Async XLA Ops:
  0.0 141.4 %copy-start = (f32[16,128]{1,0:T(8,128)S(1)}, f32[16,128]{1,0:T(8,128)}, u32[]{:S(2)}) copy-start(f32[16,128]{1,0:T(8,128)} %param.8) | copy-start | bytes 24580
  1.5 11.4 %all-to-all-start.2 = ((bf16[4,2,128]{2,1,0:T(2,128)(2,1)}), bf16[4,2,128]{2,1,0:T(2,128)(2,1)S(1)}, u32[]{:S(2)}, u32[]{:S(2)}) async-start(bf16[4,2,128]{2,1,0:T(2,128)(2,1)} %reshape.93), calls=%async_computation.2 | async-start | bytes 4096 | tf_op jit(solution)/shard_map/all_to_all | solution.py:67
  12.9 5.0 %copy-start.2 = (s32[4,16,128]{2,1,0:T(8,128)S(1)}, s32[4,16,128]{2,1,0:T(8,128)}, u32[]{:S(2)}) copy-start(s32[4,16,128]{2,1,0:T(8,128)} %param.7) | copy-start | bytes 98308
  12.9 52.5 %all-to-all-start = ((bf16[4,16,256,128]{3,2,0,1:T(8,128)(2,1)}), bf16[4,16,256,128]{3,2,0,1:T(8,128)(2,1)}, u32[]{:S(2)}, u32[]{:S(2)}) async-start(bf16[4,16,256,128]{3,2,0,1:T(8,128)(2,1)} %copy_convert_fusion), calls=%async_computation | async-start | bytes 8388608 | tf_op jit(solution)/shard_map/all_to_all | solution.py:66
  65.4 56.7 %all-to-all-start.3 = ((bf16[64,1,16]{2,1,0:T(2,128)(2,1)}), bf16[64,1,16]{2,1,0:T(2,128)(2,1)S(1)}, u32[]{:S(2)}, u32[]{:S(2)}) async-start(bf16[64,1,16]{2,1,0:T(2,128)(2,1)} %copy.144), calls=%async_computation.3 | async-start | bytes 65536 | tf_op jit(solution)/shard_map/all_to_all | solution.py:75
  81.6 39.9 %copy-start.1 = (bf16[4,4,4,256,128]{4,3,2,1,0:T(8,128)(2,1)}, bf16[4,4,4,256,128]{4,3,2,1,0:T(8,128)(2,1)S(1)}, u32[]{:S(2)}) copy-start(bf16[4,4,4,256,128]{4,3,2,1,0:T(8,128)(2,1)S(1)} %copy.140) | copy-start | bytes 12582916
  122.1 7.4 %all-to-all-start.4 = ((bf16[4,16,128]{2,0,1:T(4,128)(2,1)}), bf16[4,16,128]{2,0,1:T(4,128)(2,1)S(1)}, u32[]{:S(2)}, u32[]{:S(2)}) async-start(bf16[4,16,128]{2,0,1:T(4,128)(2,1)} %copy_convert_fusion.1), calls=%async_computation.4 | async-start | bytes 32768 | tf_op jit(solution)/shard_map/all_to_all | solution.py:68
  126.9 15.1 %copy-start.3 = (f32[128]{0:T(128)S(1)}, f32[128]{0:T(128)}, u32[]{:S(2)}) copy-start(f32[128]{0:T(128)} %param.9) | copy-start | bytes 1540
  129.6 107.5 %all-to-all-start.1 = ((bf16[64,1,256,128]{3,2,1,0:T(8,128)(2,1)}), bf16[64,1,256,128]{3,2,1,0:T(8,128)(2,1)}, u32[]{:S(2)}, u32[]{:S(2)}) async-start(bf16[64,1,256,128]{3,2,1,0:T(8,128)(2,1)} %constant_dynamic-update-slice_fusion), calls=%async_computation.1 | async-start | bytes 8388608 | tf_op jit(solution)/shard_map/all_to_all | solution.py:54
